TPU v7x, 32 devices: a whole 2x2x4 slice. The times are simulated.
32 devices in a mesh: clusters: 2 (over x), blk: 16 (over z, y, core).
Axes of the slice: x: 2, y: 2, z: 4, core: 2. Of those that a mesh axis runs over, the one named last changes fastest.
Arguments:
- positions: float32 [3, 65536], P(None, ('clusters', 'blk')), parts along dimension 1, may hold values from -6 to 6
- velocities: float32 [3, 65536], P(None, ('clusters', 'blk')), parts along dimension 1, may hold values from -6 to 6
- masses: float32 [65536], P(('clusters', 'blk')), parts along dimension 0, may hold values from 0.000390625 to 0.00390625
- active: int32 [8192], P(('clusters', 'blk')), parts along dimension 0, may hold values from 0 to 32767, as said below
Outputs:
- new_positions: float32 [3, 8192], P(None, ('clusters', 'blk')), parts along dimension 1
- new_velocities: float32 [3, 8192], P(None, ('clusters', 'blk')), parts along dimension 1
- accelerations: float32 [3, 8192], P(None, ('clusters', 'blk')), parts along dimension 1
- jerks: float32 [3, 8192], P(None, ('clusters', 'blk')), parts along dimension 1
There are 2 independent parts, one for each index of `clusters`. A program takes and returns all parts, laid end to end along the dimension named above; each array names one. Nothing has to cross between parts.
Inputs may be any that keep to these rules, and one draw needn't show every extreme that they name: Entries b * 256 to (b + 1) * 256 - 1 of active name distinct stars among b * 2048 to (b + 1) * 2048 - 1, for every block b.
All inputs are finite; a program needn't handle non-finite values.
Results may differ from a plain program's by a relative error of at most 0.00023.
Values sent between devices are 32-bit elements; how exact they have to be, the bound alone decides.
A program may use at most 64 MiB of HBM per device.

v0:
```python
import jax
import jax.numpy as jnp
from jax import lax
from jax.sharding import PartitionSpec as P

STEPS = 2


def pair_terms(target_pos, target_vel, source):
    separation = source[0:3, None, :] - target_pos[:, :, None]
    closing = source[3:6, None, :] - target_vel[:, :, None]
    squared = jnp.sum(separation * separation, axis=0) + 0.0025
    inverse = lax.rsqrt(squared)
    weight = source[6][None, :] * inverse * inverse * inverse
    radial = jnp.sum(separation * closing, axis=0)
    accel = jnp.sum(weight[None] * separation, axis=-1)
    jerk = jnp.sum(weight[None] * (closing - 3.0 * (radial / squared)[None] * separation), axis=-1)
    return (accel, jerk)


def add_piece(carry, target_pos, target_vel, source, widest):
    count = source.shape[1]
    block_len = min(count, widest)
    while count % block_len != 0:
        block_len = block_len - 1

    def add_block(totals, block):
        accel, jerk = pair_terms(target_pos, target_vel, block)
        return (totals[0] + accel, totals[1] + jerk)

    blocks = source.reshape(7, count // block_len, block_len).transpose(1, 0, 2)

    def scan_step(totals, block):
        return (add_block(totals, block), None)

    carry, unused = lax.scan(scan_step, carry, blocks)
    return carry


def shards(positions, velocities, masses, active):
    time_step = 0.03125
    local_idx = active - lax.axis_index("blk") * positions.shape[1]
    pos = jnp.take(positions, local_idx, axis=1)
    vel = jnp.take(velocities, local_idx, axis=1)
    mass = jnp.take(masses, local_idx, axis=0)
    zeros = jnp.zeros(pos.shape, jnp.float32)

    def field(pred_pos, pred_vel):
        packed = jnp.concatenate([pred_pos, pred_vel, mass[None, :]], axis=0)
        return add_piece(
            (zeros, zeros),
            pred_pos,
            pred_vel,
            lax.all_gather(packed, "blk", axis=1, tiled=True),
            2048,
        )

    accel, jerk = field(pos, vel)
    for section in range(STEPS):
        pred_pos = pos + time_step * vel + time_step**2 / 2.0 * accel + time_step**3 / 6.0 * jerk
        pred_vel = vel + time_step * accel + time_step**2 / 2.0 * jerk
        accel_new, jerk_new = field(pred_pos, pred_vel)
        vel_new = (
            vel + time_step / 2.0 * (accel + accel_new) + time_step**2 / 12.0 * (jerk - jerk_new)
        )
        pos_new = (
            pos + time_step / 2.0 * (vel + vel_new) + time_step**2 / 12.0 * (accel - accel_new)
        )
        pos, vel, accel, jerk = (pos_new, vel_new, accel_new, jerk_new)
    return (pos, vel, accel, jerk)


def solution(mesh):
    in_specs = (
        P(None, ("clusters", "blk")),
        P(None, ("clusters", "blk")),
        P(("clusters", "blk")),
        P(("clusters", "blk")),
    )
    out_specs = (
        P(None, ("clusters", "blk")),
        P(None, ("clusters", "blk")),
        P(None, ("clusters", "blk")),
        P(None, ("clusters", "blk")),
    )
    return jax.shard_map(shards, mesh=mesh, in_specs=in_specs, out_specs=out_specs, check_vma=False)
```

profile of v0, /device:TPU:0, one launch (start us, length us, event | category | flops | bytes accessed | tf_op | source)
XLA Modules:
  0.0 118.5 jit_solution(10779537461576853421)
XLA Ops:
  6.9 23.5 %all_gather.9 = f32[7,4096]{1,0:T(8,128)S(1)} all-gather(f32[7,256]{1,0:T(8,128)S(1)} %pad_maximum_fusion.2), channel_id=1, replica_groups=mesh['clusters'=2,'blk'=16] {'blk'}, dimensions={1}, use_global_device_ids=true | all-gather | bytes 121856 | tf_op jit(solution)/shard_map/all_gather | solution.py:54
  30.4 16.8 %while.39 = (s32[]{:T(128)}, f32[3,256]{1,0:T(4,128)S(1)}, f32[3,256]{1,0:T(4,128)S(1)}, f32[2,7,2048]{2,1,0:T(8,128)S(1)}, f32[3,256]{1,0:T(4,128)S(1)}, /*inde...) while((s32[]{:T(128)}, f32[3,256]{1,0:T(4,128)S(1)}, f32[3,256]{1,0:T(4,128)S(1)}, ...), condition=%wide.region_5.7_spmd.clone, body=%wide.region_0.6_spmd.clone.sunk | while | flops 24118788 | bytes 17035412 | solution.py:36
  30.4 3.6 %fusion.21 = (f32[256,2048]{1,0:T(8,128)S(1)}, f32[256,2048]{1,0:T(8,128)}) fusion(f32[3,256]{1,0:T(4,128)S(1)} %get-tuple-element.533, f32[3,2048]{1,0:T(4,128)S(1)} %get-tuple-element.466, f32[3,256]{1,0:T(4,128)S(1)} %get-tuple-element.532, f32[3,2048]{1,0:T(4,128)S(1)} %get-tuple-element.467), kind=kLoop, calls=%fused_computation.12.clone.1 | loop fusion | flops 8388608 | bytes 4249600 | tf_op jit(solution)/shard_map/while/body/eval_jaxpr/reduce_sum | solution.py:15
  34.0 2.4 %multiply_multiply_fusion.6 = (f32[256,2048]{1,0:T(8,128)S(1)}, f32[256,2048]{1,0:T(8,128)S(1)}) fusion(f32[256,2048]{1,0:T(8,128)} %get-tuple-element.468, f32[2048]{0:T(1024)S(1)} %bitcast.44, f32[256,2048]{1,0:T(8,128)S(1)} %get-tuple-element.469), kind=kLoop, calls=%fused_computation.13.clone.1 | loop fusion | flops 3145728 | bytes 8396800 | tf_op jit(solution)/shard_map/while/body/eval_jaxpr/mul | solution.py:14
  36.4 2.4 %fusion.22 = (f32[3,256]{1,0:T(4,128)S(1)}, f32[3,256]{1,0:T(4,128)S(1)}) fusion(f32[256,2048]{1,0:T(8,128)S(1)} %get-tuple-element.470, f32[3,256]{1,0:T(4,128)S(1)} %get-tuple-element.533, f32[3,2048]{1,0:T(4,128)S(1)} %get-tuple-element.466, f32[256,2048]{1,0:T(8,128)S(1)} %get-tuple-element.471, f32[3,256]{1,0:T(4,128)S(1)} %get-tuple-element.532, ...), kind=kLoop, calls=%fused_computation.9.clone.1 | loop fusion | flops 12581376 | bytes 4255744 | tf_op jit(solution)/shard_map/while/body/eval_jaxpr/reduce_sum | solution.py:17
  38.9 3.6 %fusion.21 = (f32[256,2048]{1,0:T(8,128)S(1)}, f32[256,2048]{1,0:T(8,128)}) fusion(f32[3,256]{1,0:T(4,128)S(1)} %get-tuple-element.533, f32[3,2048]{1,0:T(4,128)S(1)} %get-tuple-element.466, f32[3,256]{1,0:T(4,128)S(1)} %get-tuple-element.532, f32[3,2048]{1,0:T(4,128)S(1)} %get-tuple-element.467), kind=kLoop, calls=%fused_computation.12.clone.1 | loop fusion | flops 8388608 | bytes 4249600 | tf_op jit(solution)/shard_map/while/body/eval_jaxpr/reduce_sum | solution.py:15
  42.4 2.4 %multiply_multiply_fusion.6 = (f32[256,2048]{1,0:T(8,128)S(1)}, f32[256,2048]{1,0:T(8,128)S(1)}) fusion(f32[256,2048]{1,0:T(8,128)} %get-tuple-element.468, f32[2048]{0:T(1024)S(1)} %bitcast.44, f32[256,2048]{1,0:T(8,128)S(1)} %get-tuple-element.469), kind=kLoop, calls=%fused_computation.13.clone.1 | loop fusion | flops 3145728 | bytes 8396800 | tf_op jit(solution)/shard_map/while/body/eval_jaxpr/mul | solution.py:14
  44.8 2.4 %fusion.22 = (f32[3,256]{1,0:T(4,128)S(1)}, f32[3,256]{1,0:T(4,128)S(1)}) fusion(f32[256,2048]{1,0:T(8,128)S(1)} %get-tuple-element.470, f32[3,256]{1,0:T(4,128)S(1)} %get-tuple-element.533, f32[3,2048]{1,0:T(4,128)S(1)} %get-tuple-element.466, f32[256,2048]{1,0:T(8,128)S(1)} %get-tuple-element.471, f32[3,256]{1,0:T(4,128)S(1)} %get-tuple-element.532, ...), kind=kLoop, calls=%fused_computation.9.clone.1 | loop fusion | flops 12581376 | bytes 4255744 | tf_op jit(solution)/shard_map/while/body/eval_jaxpr/reduce_sum | solution.py:17
  47.3 17.8 %all_gather.10 = f32[7,4096]{1,0:T(8,128)S(1)} all-gather(f32[7,256]{1,0:T(8,128)S(1)} %pad_maximum_fusion.1), channel_id=1, replica_groups=mesh['clusters'=2,'blk'=16] {'blk'}, dimensions={1}, use_global_device_ids=true | all-gather | bytes 121856 | tf_op jit(solution)/shard_map/all_gather | solution.py:54
  65.1 16.8 %while.40 = (s32[]{:T(128)}, f32[3,256]{1,0:T(4,128)S(1)}, f32[3,256]{1,0:T(4,128)S(1)}, f32[2,7,2048]{2,1,0:T(8,128)S(1)}, f32[3,256]{1,0:T(4,128)S(1)}, /*inde...) while((s32[]{:T(128)}, f32[3,256]{1,0:T(4,128)S(1)}, f32[3,256]{1,0:T(4,128)S(1)}, ...), condition=%wide.region_11.13_spmd.clone, body=%wide.region_6.12_spmd.clone.sunk | while | flops 24118788 | bytes 17035412 | solution.py:36
  65.1 3.6 %fusion.23 = (f32[256,2048]{1,0:T(8,128)S(1)}, f32[256,2048]{1,0:T(8,128)}) fusion(f32[3,256]{1,0:T(4,128)S(1)} %get-tuple-element.563, f32[3,2048]{1,0:T(4,128)S(1)} %get-tuple-element.482, f32[3,256]{1,0:T(4,128)S(1)} %get-tuple-element.562, f32[3,2048]{1,0:T(4,128)S(1)} %get-tuple-element.483), kind=kLoop, calls=%fused_computation.29.clone.1 | loop fusion | flops 8388608 | bytes 4249600 | tf_op jit(solution)/shard_map/while/body/eval_jaxpr/reduce_sum | solution.py:15
  68.7 2.4 %multiply_multiply_fusion.7 = (f32[256,2048]{1,0:T(8,128)S(1)}, f32[256,2048]{1,0:T(8,128)S(1)}) fusion(f32[256,2048]{1,0:T(8,128)} %get-tuple-element.484, f32[2048]{0:T(1024)S(1)} %bitcast.45, f32[256,2048]{1,0:T(8,128)S(1)} %get-tuple-element.485), kind=kLoop, calls=%fused_computation.30.clone.1 | loop fusion | flops 3145728 | bytes 8396800 | tf_op jit(solution)/shard_map/while/body/eval_jaxpr/mul | solution.py:14
  71.0 2.4 %fusion.24 = (f32[3,256]{1,0:T(4,128)S(1)}, f32[3,256]{1,0:T(4,128)S(1)}) fusion(f32[256,2048]{1,0:T(8,128)S(1)} %get-tuple-element.486, f32[3,256]{1,0:T(4,128)S(1)} %get-tuple-element.563, f32[3,2048]{1,0:T(4,128)S(1)} %get-tuple-element.482, f32[256,2048]{1,0:T(8,128)S(1)} %get-tuple-element.487, f32[3,256]{1,0:T(4,128)S(1)} %get-tuple-element.562, ...), kind=kLoop, calls=%fused_computation.26.clone.1 | loop fusion | flops 12581376 | bytes 4255744 | tf_op jit(solution)/shard_map/while/body/eval_jaxpr/reduce_sum | solution.py:17
  73.5 3.6 %fusion.23 = (f32[256,2048]{1,0:T(8,128)S(1)}, f32[256,2048]{1,0:T(8,128)}) fusion(f32[3,256]{1,0:T(4,128)S(1)} %get-tuple-element.563, f32[3,2048]{1,0:T(4,128)S(1)} %get-tuple-element.482, f32[3,256]{1,0:T(4,128)S(1)} %get-tuple-element.562, f32[3,2048]{1,0:T(4,128)S(1)} %get-tuple-element.483), kind=kLoop, calls=%fused_computation.29.clone.1 | loop fusion | flops 8388608 | bytes 4249600 | tf_op jit(solution)/shard_map/while/body/eval_jaxpr/reduce_sum | solution.py:15
  77.1 2.4 %multiply_multiply_fusion.7 = (f32[256,2048]{1,0:T(8,128)S(1)}, f32[256,2048]{1,0:T(8,128)S(1)}) fusion(f32[256,2048]{1,0:T(8,128)} %get-tuple-element.484, f32[2048]{0:T(1024)S(1)} %bitcast.45, f32[256,2048]{1,0:T(8,128)S(1)} %get-tuple-element.485), kind=kLoop, calls=%fused_computation.30.clone.1 | loop fusion | flops 3145728 | bytes 8396800 | tf_op jit(solution)/shard_map/while/body/eval_jaxpr/mul | solution.py:14
  79.4 2.4 %fusion.24 = (f32[3,256]{1,0:T(4,128)S(1)}, f32[3,256]{1,0:T(4,128)S(1)}) fusion(f32[256,2048]{1,0:T(8,128)S(1)} %get-tuple-element.486, f32[3,256]{1,0:T(4,128)S(1)} %get-tuple-element.563, f32[3,2048]{1,0:T(4,128)S(1)} %get-tuple-element.482, f32[256,2048]{1,0:T(8,128)S(1)} %get-tuple-element.487, f32[3,256]{1,0:T(4,128)S(1)} %get-tuple-element.562, ...), kind=kLoop, calls=%fused_computation.26.clone.1 | loop fusion | flops 12581376 | bytes 4255744 | tf_op jit(solution)/shard_map/while/body/eval_jaxpr/reduce_sum | solution.py:17
  81.9 19.1 %all_gather.11 = f32[7,4096]{1,0:T(8,128)S(1)} all-gather(f32[7,256]{1,0:T(8,128)S(1)} %pad_maximum_fusion), channel_id=1, replica_groups=mesh['clusters'=2,'blk'=16] {'blk'}, dimensions={1}, use_global_device_ids=true | all-gather | bytes 121856 | tf_op jit(solution)/shard_map/all_gather | solution.py:54
  101.1 16.8 %while.41 = (s32[]{:T(128)}, f32[3,256]{1,0:T(4,128)S(1)}, f32[3,256]{1,0:T(4,128)S(1)}, f32[2,7,2048]{2,1,0:T(8,128)S(1)}, f32[3,256]{1,0:T(4,128)S(1)}, /*inde...) while((s32[]{:T(128)}, f32[3,256]{1,0:T(4,128)S(1)}, f32[3,256]{1,0:T(4,128)S(1)}, ...), condition=%wide.region_17.19_spmd.clone, body=%wide.region_12.18_spmd.clone.sunk | while | flops 24118788 | bytes 17035412 | solution.py:36
  101.1 3.6 %fusion.25 = (f32[256,2048]{1,0:T(8,128)S(1)}, f32[256,2048]{1,0:T(8,128)}) fusion(f32[3,256]{1,0:T(4,128)S(1)} %get-tuple-element.593, f32[3,2048]{1,0:T(4,128)S(1)} %get-tuple-element.498, f32[3,256]{1,0:T(4,128)S(1)} %get-tuple-element.592, f32[3,2048]{1,0:T(4,128)S(1)} %get-tuple-element.499), kind=kLoop, calls=%fused_computation.46.clone.1 | loop fusion | flops 8388608 | bytes 4249600 | tf_op jit(solution)/shard_map/while/body/eval_jaxpr/reduce_sum | solution.py:15
  104.7 2.4 %multiply_multiply_fusion.8 = (f32[256,2048]{1,0:T(8,128)S(1)}, f32[256,2048]{1,0:T(8,128)S(1)}) fusion(f32[256,2048]{1,0:T(8,128)} %get-tuple-element.500, f32[2048]{0:T(1024)S(1)} %bitcast.46, f32[256,2048]{1,0:T(8,128)S(1)} %get-tuple-element.501), kind=kLoop, calls=%fused_computation.47.clone.1 | loop fusion | flops 3145728 | bytes 8396800 | tf_op jit(solution)/shard_map/while/body/eval_jaxpr/mul | solution.py:14
  107.0 2.4 %fusion.26 = (f32[3,256]{1,0:T(4,128)S(1)}, f32[3,256]{1,0:T(4,128)S(1)}) fusion(f32[256,2048]{1,0:T(8,128)S(1)} %get-tuple-element.502, f32[3,256]{1,0:T(4,128)S(1)} %get-tuple-element.593, f32[3,2048]{1,0:T(4,128)S(1)} %get-tuple-element.498, f32[256,2048]{1,0:T(8,128)S(1)} %get-tuple-element.503, f32[3,256]{1,0:T(4,128)S(1)} %get-tuple-element.592, ...), kind=kLoop, calls=%fused_computation.43.clone.1 | loop fusion | flops 12581376 | bytes 4255744 | tf_op jit(solution)/shard_map/while/body/eval_jaxpr/reduce_sum | solution.py:17
  109.5 3.6 %fusion.25 = (f32[256,2048]{1,0:T(8,128)S(1)}, f32[256,2048]{1,0:T(8,128)}) fusion(f32[3,256]{1,0:T(4,128)S(1)} %get-tuple-element.593, f32[3,2048]{1,0:T(4,128)S(1)} %get-tuple-element.498, f32[3,256]{1,0:T(4,128)S(1)} %get-tuple-element.592, f32[3,2048]{1,0:T(4,128)S(1)} %get-tuple-element.499), kind=kLoop, calls=%fused_computation.46.clone.1 | loop fusion | flops 8388608 | bytes 4249600 | tf_op jit(solution)/shard_map/while/body/eval_jaxpr/reduce_sum | solution.py:15
  113.1 2.4 %multiply_multiply_fusion.8 = (f32[256,2048]{1,0:T(8,128)S(1)}, f32[256,2048]{1,0:T(8,128)S(1)}) fusion(f32[256,2048]{1,0:T(8,128)} %get-tuple-element.500, f32[2048]{0:T(1024)S(1)} %bitcast.46, f32[256,2048]{1,0:T(8,128)S(1)} %get-tuple-element.501), kind=kLoop, calls=%fused_computation.47.clone.1 | loop fusion | flops 3145728 | bytes 8396800 | tf_op jit(solution)/shard_map/while/body/eval_jaxpr/mul | solution.py:14
  115.4 2.4 %fusion.26 = (f32[3,256]{1,0:T(4,128)S(1)}, f32[3,256]{1,0:T(4,128)S(1)}) fusion(f32[256,2048]{1,0:T(8,128)S(1)} %get-tuple-element.502, f32[3,256]{1,0:T(4,128)S(1)} %get-tuple-element.593, f32[3,2048]{1,0:T(4,128)S(1)} %get-tuple-element.498, f32[256,2048]{1,0:T(8,128)S(1)} %get-tuple-element.503, f32[3,256]{1,0:T(4,128)S(1)} %get-tuple-element.592, ...), kind=kLoop, calls=%fused_computation.43.clone.1 | loop fusion | flops 12581376 | bytes 4255744 | tf_op jit(solution)/shard_map/while/body/eval_jaxpr/reduce_sum | solution.py:17
  (49 shorter events, 7.2 us)
Async XLA Ops:
  0.6 0.7 copy-start
  0.6 5.1 %copy-start.3 = (f32[3,2048]{1,0:T(4,128)S(1)}, f32[3,2048]{1,0:T(4,128)}, u32[]{:S(2)}) copy-start(f32[3,2048]{1,0:T(4,128)} %param.13) | copy-start | bytes 73732
  117.9 0.6 copy-start.1
  117.9 0.6 copy-start.2
where the time goes:
time: 119 us
  blocking collectives  60.4 us (51%)
  other arithmetic  52.1 us (44%)
  local copies, waits for them, and re-layouts  5.04 us (4%)
    all_gather x3, blocking collectives, field(): lax.all_gather(packed, 'blk', axis=1, tiled=True)  60.4 us
    reduce_sum x6, other arithmetic, pair_terms(): radial = jnp.sum(separation * closing, axis=0)  21.4 us
    reduce_sum x6, other arithmetic, pair_terms(): jnp.sum(weight[None] * (closing - 3.0 * (radial / squared)[None] * separa...  14.4 us
    mul x6, other arithmetic, pair_terms(): weight = source[6][None, :] * inverse * inverse * inverse  14.1 us

commit v1 on v0

v1 whole, which is shorter than its diff:
```python
import functools

import jax
import jax.numpy as jnp
from jax import lax
from jax.experimental import pallas as pl
from jax.experimental.pallas import tpu as pltpu
from jax.sharding import PartitionSpec as P

STEPS = 2
TIME_STEP = 0.03125
ROWS = 32
F32 = jnp.float32
BF16 = jnp.bfloat16


def split3(value):
    high = value.astype(BF16)
    rest = value - high.astype(F32)
    middle = rest.astype(BF16)
    low = (rest - middle.astype(F32)).astype(BF16)
    return [high, middle, low]


def kernel(
    n,
    pos_ref,
    vel_ref,
    mass_ref,
    idx_ref,
    pos_out,
    vel_out,
    accel_out,
    jerk_out,
    slots,
    target,
    even,
    odd,
    right_even,
    right_odd,
    total,
    send_sem,
    recv_sem,
):
    me = lax.axis_index("blk")
    act = idx_ref.shape[1]
    stars = pos_ref.shape[1]

    def peer_of(j):
        offset = ((j + 1) // 2) * (2 * (j % 2) - 1)
        return (me + offset + n) % n

    barrier = pltpu.get_barrier_semaphore()

    @pl.loop(1, n)
    def _(j):
        pl.semaphore_signal(
            barrier,
            inc=1,
            device_id={"blk": peer_of(j)},
            device_id_type=pl.DeviceIdType.MESH,
        )

    local_idx = idx_ref[...] - me * stars
    table = jnp.concatenate(
        [pos_ref[...], vel_ref[...], mass_ref[...], jnp.zeros((1, stars), F32)], axis=0
    )
    pieces = jnp.concatenate(split3(table), axis=0)
    picked = (lax.broadcasted_iota(jnp.int32, (stars, act), 0) == local_idx).astype(F32).astype(BF16)
    found = jnp.dot(pieces, picked, preferred_element_type=F32)
    own = found[0:8] + found[8:16] + found[16:24]
    mass_rows = own[6:8]

    pl.semaphore_wait(barrier, n - 1)

    def copy_to(step, j):
        return pltpu.make_async_remote_copy(
            src_ref=slots.at[step, me],
            dst_ref=slots.at[step, me],
            send_sem=send_sem.at[step, j],
            recv_sem=recv_sem.at[step, me],
            device_id={"blk": peer_of(j)},
            device_id_type=pl.DeviceIdType.MESH,
        )

    def wait_from(step, j):
        peer = peer_of(j)
        pltpu.make_async_remote_copy(
            src_ref=slots.at[step, peer],
            dst_ref=slots.at[step, peer],
            send_sem=send_sem.at[step, j],
            recv_sem=recv_sem.at[step, peer],
            device_id={"blk": peer},
            device_id_type=pl.DeviceIdType.MESH,
        ).wait_recv()

    row_id = lax.broadcasted_iota(jnp.int32, (8, act), 0)

    def weigh(source, weights, right, centre):
        for half in range(act // 128):
            lanes = slice(half * 128, half * 128 + 128)
            src = [source[c : c + 1, lanes] for c in range(6)]
            for top in range(0, act, ROWS):
                rows = slice(top, top + ROWS)
                d = [src[c] - target[c, rows, :] for c in range(3)]
                e = [src[c + 3] - target[c + 3, rows, :] for c in range(3)]
                squared = d[0] * d[0] + d[1] * d[1] + d[2] * d[2] + 0.0025
                radial = d[0] * e[0] + d[1] * e[1] + d[2] * e[2]
                inverse = lax.rsqrt(squared)
                inverse2 = inverse * inverse
                w = inverse2 * inverse
                b = w * inverse2 * radial
                for value, down in ((w, 0), (b, act)):
                    high = value.astype(BF16)
                    low = (value - high.astype(F32)).astype(BF16)
                    out = slice(down + top, down + top + ROWS)
                    weights[out, lanes] = high
                    weights[out, act + half * 128 : act + half * 128 + 128] = low
        factor = jnp.where(row_id == 6, 1.0, source - centre)
        splits = jnp.concatenate(split3(factor * source[6:7]), axis=0)
        right[...] = jnp.concatenate([splits, splits], axis=1)

    def gather_sums(weights, right):
        total[...] += lax.dot_general(
            weights[...],
            right[...],
            (((1,), (1,)), ((), ())),
            preferred_element_type=F32,
        )

    def field(step, own):
        slots[step, me] = own

        @pl.loop(1, n)
        def _(k):
            copy_to(step, n - k).start()

        columns = own.T
        for c in range(6):
            target[c] = jnp.broadcast_to(columns[:, c : c + 1], (act, 128))
        centre = jnp.where(row_id[:, 0:1] < 6, jnp.mean(own, axis=1, keepdims=True), 0.0)
        total[...] = jnp.zeros_like(total)
        odd[...] = jnp.zeros_like(odd)
        right_odd[...] = jnp.zeros_like(right_odd)

        @pl.loop(0, n // 2)
        def _(pair):
            first = 2 * pair

            @pl.when(pair > 0)
            def _():
                wait_from(step, first)

            wait_from(step, first + 1)
            gather_sums(odd, right_odd)
            weigh(slots[step, peer_of(first)], even, right_even, centre)
            gather_sums(even, right_even)
            weigh(slots[step, peer_of(first + 1)], odd, right_odd, centre)

        gather_sums(odd, right_odd)
        sums = total[...].T
        sums = sums[0:8] + sums[8:16] + sums[16:24]
        plain, scaled = sums[:, 0:act], sums[:, act:]
        about = own - centre
        accel = plain[0:3] - about[0:3] * plain[6:7]
        jerk = (
            plain[3:6]
            - about[3:6] * plain[6:7]
            - 3.0 * (scaled[0:3] - about[0:3] * scaled[6:7])
        )
        return accel, jerk

    pos, vel = own[0:3], own[3:6]
    accel, jerk = field(0, own)
    h = TIME_STEP
    for step in range(STEPS):
        pred_pos = pos + h * vel + h**2 / 2.0 * accel + h**3 / 6.0 * jerk
        pred_vel = vel + h * accel + h**2 / 2.0 * jerk
        accel_new, jerk_new = field(
            step + 1, jnp.concatenate([pred_pos, pred_vel, mass_rows], axis=0)
        )
        vel_new = vel + h / 2.0 * (accel + accel_new) + h**2 / 12.0 * (jerk - jerk_new)
        pos = pos + h / 2.0 * (vel + vel_new) + h**2 / 12.0 * (accel - accel_new)
        vel, accel, jerk = vel_new, accel_new, jerk_new
    pos_out[...] = pos
    vel_out[...] = vel
    accel_out[...] = accel
    jerk_out[...] = jerk

    for step in range(STEPS + 1):

        @pl.loop(1, n)
        def _(j):
            copy_to(step, j).wait_send()


def solution(mesh):
    n = mesh.shape["blk"]

    def shards(positions, velocities, masses, active):
        act = active.shape[0]
        vmem = pl.BlockSpec(memory_space=pltpu.VMEM)
        return pl.pallas_call(
            functools.partial(kernel, n),
            out_shape=[jax.ShapeDtypeStruct((3, act), F32)] * 4,
            in_specs=[vmem] * 4,
            out_specs=[vmem] * 4,
            scratch_shapes=[
                pltpu.VMEM((STEPS + 1, n, 8, act), F32),
                pltpu.VMEM((6, act, 128), F32),
                pltpu.VMEM((2 * act, 2 * act), BF16),
                pltpu.VMEM((2 * act, 2 * act), BF16),
                pltpu.VMEM((24, 2 * act), BF16),
                pltpu.VMEM((24, 2 * act), BF16),
                pltpu.VMEM((2 * act, 24), F32),
                pltpu.SemaphoreType.DMA((STEPS + 1, n)),
                pltpu.SemaphoreType.DMA((STEPS + 1, n)),
            ],
            compiler_params=pltpu.CompilerParams(collective_id=0, has_side_effects=True),
        )(positions, velocities, masses.reshape(1, -1), active.reshape(1, -1))

    spec = P(None, ("clusters", "blk"))
    flat = P(("clusters", "blk"))
    return jax.shard_map(
        shards,
        mesh=mesh,
        in_specs=(spec, spec, flat, flat),
        out_specs=(spec, spec, spec, spec),
        check_vma=False,
    )
```

time: 119 us -> 46.4 us (0.39)
  blocking collectives: 60.4 us -> 0 us
  other arithmetic: 52.1 us -> 0 us
  Pallas kernels: 0 us -> 42.1 us
  local copies, waits for them, and re-layouts: 5.04 us -> 3.3 us
    all_gather x3 -> x0, blocking collectives: 60.4 us -> none  [field(): lax.all_gather(packed, 'blk', axis=1, tiled=True)]
    pallas_call x0 -> x1, Pallas kernels: none -> 42.1 us  [shards(): pl.pallas_call(functools.partial(kernel, n), out_shape=[jax.ShapeDtypeStr...]
    reduce_sum x12 -> x0, other arithmetic: 35.8 us -> none  [the longest x6 21.4 us: pair_terms(): radial = jnp.sum(separation * closing, axis=0)]
    mul x6 -> x0, other arithmetic: 14.1 us -> none  [pair_terms(): weight = source[6][None, :] * inverse * inverse * inverse]
    gather x5 -> x0, local copies, waits for them, and re-layouts: 3.34 us -> none  [the longest x1 1.72 us: shards(): mass = jnp.take(masses, local_idx, axis=0)]
    unnamed x10 -> x12, local copies, waits for them, and re-layouts: 1.51 us -> 3.3 us
    select_n x3 -> x0, other arithmetic: 1.39 us -> none  [the longest x2 0.7 us: shards(): pos = jnp.take(positions, local_idx, axis=1)]
where the time goes in v1:
time: 46.4 us; the launch traced here: 46.1 us
  Pallas kernels  42.1 us (91%)
  local copies, waits for them, and re-layouts  3.3 us (7%)
  between operations  0.65 us (1%)
    pallas_call x1, Pallas kernels, shards(): pl.pallas_call(functools.partial(kernel, n), out_shape=[jax.ShapeDtypeStr...  42.1 us
    unnamed x12, local copies, waits for them, and re-layouts  3.3 us

profile of v1, /device:TPU:0, one launch (start us, length us, event | category | flops | bytes accessed | tf_op | source)
XLA Modules:
  0.0 46.1 jit_solution(13991903582635086650)
XLA Ops:
  0.6 42.1 %shard_map.75 = (f32[3,256]{1,0:T(4,128)}, f32[3,256]{1,0:T(4,128)}, f32[3,256]{1,0:T(4,128)}, f32[3,256]{1,0:T(4,128)}) custom-call(f32[3,2048]{1,0:T(4,128)} %pos_ref.1, f32[3,2048]{1,0:T(4,128)} %vel_ref.1, f32[1,2048]{1,0:T(1,128)} %bitcast.2, s32[1,256]{1,0:T(1,128)} %bitcast.3), custom_call_target="tpu_custom_call" | custom-call | tf_op jit(solution)/shard_map/pallas_call | solution.py:203
  42.8 0.0 copy-start.3
  42.8 0.7 %copy-done.3 = f32[3,256]{1,0:T(4,128)S(1)} copy-done((f32[3,256]{1,0:T(4,128)S(1)}, f32[3,256]{1,0:T(4,128)}, u32[]{:S(2)}) %copy-start.3) | copy-done | bytes 3096
  43.4 0.0 copy-start.2
  43.4 0.6 %copy.12 = f32[3,256]{1,0:T(4,128)} copy(f32[3,256]{1,0:T(4,128)S(1)} %copy-done.3) | data formatting | bytes 6144
  44.0 0.1 copy-done.2
  44.1 0.0 copy-start.1
  44.1 0.6 %copy.13 = f32[3,256]{1,0:T(4,128)} copy(f32[3,256]{1,0:T(4,128)S(1)} %copy-done.2) | data formatting | bytes 6144
  44.7 0.1 copy-done.1
  44.8 0.0 copy-start
  44.8 0.6 %copy.14 = f32[3,256]{1,0:T(4,128)} copy(f32[3,256]{1,0:T(4,128)S(1)} %copy-done.1) | data formatting | bytes 6144
  45.4 0.1 copy-done
  45.5 0.6 %copy.15 = f32[3,256]{1,0:T(4,128)} copy(f32[3,256]{1,0:T(4,128)S(1)} %copy-done) | data formatting | bytes 6144
Async XLA Ops:
  42.8 0.7 %copy-start.3 = (f32[3,256]{1,0:T(4,128)S(1)}, f32[3,256]{1,0:T(4,128)}, u32[]{:S(2)}) copy-start(f32[3,256]{1,0:T(4,128)} %get-tuple-element.8) | copy-start | bytes 9220
  43.4 0.7 %copy-start.2 = (f32[3,256]{1,0:T(4,128)S(1)}, f32[3,256]{1,0:T(4,128)}, u32[]{:S(2)}) copy-start(f32[3,256]{1,0:T(4,128)} %get-tuple-element.9) | copy-start | bytes 9220
  44.1 0.7 %copy-start.1 = (f32[3,256]{1,0:T(4,128)S(1)}, f32[3,256]{1,0:T(4,128)}, u32[]{:S(2)}) copy-start(f32[3,256]{1,0:T(4,128)} %get-tuple-element.10) | copy-start | bytes 9220
  44.8 0.7 %copy-start = (f32[3,256]{1,0:T(4,128)S(1)}, f32[3,256]{1,0:T(4,128)}, u32[]{:S(2)}) copy-start(f32[3,256]{1,0:T(4,128)} %get-tuple-element.11) | copy-start | bytes 9220

commit v2 on v1

--- a/solution.py
+++ b/solution.py
@@ -28,10 +28,7 @@
     vel_ref,
     mass_ref,
     idx_ref,
-    pos_out,
-    vel_out,
-    accel_out,
-    jerk_out,
+    out_ref,
     slots,
     target,
     even,
@@ -46,18 +43,33 @@
     act = idx_ref.shape[1]
     stars = pos_ref.shape[1]
 
-    def peer_of(j):
-        offset = ((j + 1) // 2) * (2 * (j % 2) - 1)
-        return (me + offset + n) % n
+    half = n // 2
+    core = me % 2
+
+    def same_core(order):
+        offset = ((order + 1) // 2) * (2 * (order % 2) - 1)
+        return 2 * ((me // 2 + offset + half) % half) + core
+
+    def greeted(j):
+        first = (half - j) // half
+        return first * (me + 1 - 2 * core) + (1 - first) * same_core(j)
+
+    def peer_at(place):
+        third = (place + half - 1) // half
+        start = (n - place) // n
+        second = (n - place) // (n - 1) - start
+        k = place - third * (2 - third) + half * second
+        other = k // half
+        return same_core(k - other * half) + other * (1 - 2 * core)
 
     barrier = pltpu.get_barrier_semaphore()
 
-    @pl.loop(1, n)
+    @pl.loop(0, half)
     def _(j):
         pl.semaphore_signal(
             barrier,
             inc=1,
-            device_id={"blk": peer_of(j)},
+            device_id={"blk": greeted(j)},
             device_id_type=pl.DeviceIdType.MESH,
         )
 
@@ -71,34 +83,33 @@
     own = found[0:8] + found[8:16] + found[16:24]
     mass_rows = own[6:8]
 
-    pl.semaphore_wait(barrier, n - 1)
-
-    def copy_to(step, j):
+    odd[...] = jnp.zeros_like(odd)
+    pl.semaphore_wait(barrier, half)
+
+    def copy_to(step, owner, target_id, j):
         return pltpu.make_async_remote_copy(
-            src_ref=slots.at[step, me],
-            dst_ref=slots.at[step, me],
+            src_ref=slots.at[step, owner],
+            dst_ref=slots.at[step, owner],
             send_sem=send_sem.at[step, j],
-            recv_sem=recv_sem.at[step, me],
-            device_id={"blk": peer_of(j)},
+            recv_sem=recv_sem.at[step, owner],
+            device_id={"blk": target_id},
             device_id_type=pl.DeviceIdType.MESH,
         )
 
-    def wait_from(step, j):
-        peer = peer_of(j)
-        pltpu.make_async_remote_copy(
-            src_ref=slots.at[step, peer],
-            dst_ref=slots.at[step, peer],
-            send_sem=send_sem.at[step, j],
-            recv_sem=recv_sem.at[step, peer],
-            device_id={"blk": peer},
-            device_id_type=pl.DeviceIdType.MESH,
-        ).wait_recv()
+    def wait_at(step, place):
+        peer = peer_at(place)
+        copy_to(step, peer, greeted(0), 0).wait_recv()
+        order = place - 1
+
+        @pl.when((place > 1) & (place <= half))
+        def _():
+            copy_to(step, peer, greeted(0), half + order).start()
 
     row_id = lax.broadcasted_iota(jnp.int32, (8, act), 0)
 
-    def weigh(source, weights, right, centre):
-        for half in range(act // 128):
-            lanes = slice(half * 128, half * 128 + 128)
+    def weigh(source, weights, right, centre, fine):
+        for side in range(act // 128):
+            lanes = slice(side * 128, side * 128 + 128)
             src = [source[c : c + 1, lanes] for c in range(6)]
             for top in range(0, act, ROWS):
                 rows = slice(top, top + ROWS)
@@ -112,35 +123,40 @@
                 b = w * inverse2 * radial
                 for value, down in ((w, 0), (b, act)):
                     high = value.astype(BF16)
-                    low = (value - high.astype(F32)).astype(BF16)
                     out = slice(down + top, down + top + ROWS)
                     weights[out, lanes] = high
-                    weights[out, act + half * 128 : act + half * 128 + 128] = low
+                    if fine:
+                        low = (value - high.astype(F32)).astype(BF16)
+                        weights[out, act + side * 128 : act + side * 128 + 128] = low
         factor = jnp.where(row_id == 6, 1.0, source - centre)
         splits = jnp.concatenate(split3(factor * source[6:7]), axis=0)
-        right[...] = jnp.concatenate([splits, splits], axis=1)
-
-    def gather_sums(weights, right):
+        right[:, 0:act] = splits
+        if fine:
+            right[:, act:] = splits
+
+    def gather_sums(weights, right, fine):
+        depth = 2 * act if fine else act
         total[...] += lax.dot_general(
-            weights[...],
-            right[...],
+            weights[:, 0:depth],
+            right[:, 0:depth],
             (((1,), (1,)), ((), ())),
             preferred_element_type=F32,
         )
 
     def field(step, own):
+        fine = step == STEPS
         slots[step, me] = own
 
-        @pl.loop(1, n)
+        @pl.loop(0, half)
         def _(k):
-            copy_to(step, n - k).start()
+            j = half - 1 - k
+            copy_to(step, me, greeted(j), j).start()
 
         columns = own.T
         for c in range(6):
             target[c] = jnp.broadcast_to(columns[:, c : c + 1], (act, 128))
         centre = jnp.where(row_id[:, 0:1] < 6, jnp.mean(own, axis=1, keepdims=True), 0.0)
         total[...] = jnp.zeros_like(total)
-        odd[...] = jnp.zeros_like(odd)
         right_odd[...] = jnp.zeros_like(right_odd)
 
         @pl.loop(0, n // 2)
@@ -149,15 +165,15 @@
 
             @pl.when(pair > 0)
             def _():
-                wait_from(step, first)
-
-            wait_from(step, first + 1)
-            gather_sums(odd, right_odd)
-            weigh(slots[step, peer_of(first)], even, right_even, centre)
-            gather_sums(even, right_even)
-            weigh(slots[step, peer_of(first + 1)], odd, right_odd, centre)
-
-        gather_sums(odd, right_odd)
+                wait_at(step, first)
+
+            wait_at(step, first + 1)
+            gather_sums(odd, right_odd, fine)
+            weigh(slots[step, peer_at(first)], even, right_even, centre, fine)
+            gather_sums(even, right_even, fine)
+            weigh(slots[step, peer_at(first + 1)], odd, right_odd, centre, fine)
+
+        gather_sums(odd, right_odd, fine)
         sums = total[...].T
         sums = sums[0:8] + sums[8:16] + sums[16:24]
         plain, scaled = sums[:, 0:act], sums[:, act:]
@@ -182,16 +198,17 @@
         vel_new = vel + h / 2.0 * (accel + accel_new) + h**2 / 12.0 * (jerk - jerk_new)
         pos = pos + h / 2.0 * (vel + vel_new) + h**2 / 12.0 * (accel - accel_new)
         vel, accel, jerk = vel_new, accel_new, jerk_new
-    pos_out[...] = pos
-    vel_out[...] = vel
-    accel_out[...] = accel
-    jerk_out[...] = jerk
+    out_ref[...] = jnp.concatenate([pos, vel, accel, jerk], axis=0)
 
     for step in range(STEPS + 1):
 
-        @pl.loop(1, n)
+        @pl.loop(0, half)
         def _(j):
-            copy_to(step, j).wait_send()
+            copy_to(step, me, greeted(j), j).wait_send()
+
+        @pl.loop(1, half)
+        def _(order):
+            copy_to(step, same_core(order), greeted(0), half + order).wait_send()
 
 
 def solution(mesh):
@@ -200,11 +217,11 @@
     def shards(positions, velocities, masses, active):
         act = active.shape[0]
         vmem = pl.BlockSpec(memory_space=pltpu.VMEM)
-        return pl.pallas_call(
+        packed = pl.pallas_call(
             functools.partial(kernel, n),
-            out_shape=[jax.ShapeDtypeStruct((3, act), F32)] * 4,
+            out_shape=jax.ShapeDtypeStruct((12, act), F32),
             in_specs=[vmem] * 4,
-            out_specs=[vmem] * 4,
+            out_specs=vmem,
             scratch_shapes=[
                 pltpu.VMEM((STEPS + 1, n, 8, act), F32),
                 pltpu.VMEM((6, act, 128), F32),
@@ -218,6 +235,7 @@
             ],
             compiler_params=pltpu.CompilerParams(collective_id=0, has_side_effects=True),
         )(positions, velocities, masses.reshape(1, -1), active.reshape(1, -1))
+        return packed[0:3], packed[3:6], packed[6:9], packed[9:12]
 
     spec = P(None, ("clusters", "blk"))
     flat = P(("clusters", "blk"))

time: 46.4 us -> 39.7 us (0.86)
  Pallas kernels: 42.1 us -> 37.4 us
  local copies, waits for them, and re-layouts: 3.3 us -> 1.42 us
    pallas_call x1, Pallas kernels: 42.1 us -> 37.4 us  [shards(): pl.pallas_call(functools.partial(kernel, n), out_shape=jax.ShapeDtypeStru...]
    unnamed x12 -> x0, local copies, waits for them, and re-layouts: 3.3 us -> none
    slice x0 -> x1, local copies, waits for them, and re-layouts: none -> 1.42 us  [shards(): return (packed[0:3], packed[3:6], packed[6:9], packed[9:12])]
where the time goes in v2:
time: 39.7 us; the launch traced here: 39.5 us
  Pallas kernels  37.4 us (94%)
  local copies, waits for them, and re-layouts  1.42 us (4%)
  between operations  0.64 us (2%)
    pallas_call x1, Pallas kernels, shards(): pl.pallas_call(functools.partial(kernel, n), out_shape=jax.ShapeDtypeStru...  37.4 us
    slice x1, local copies, waits for them, and re-layouts, shards(): return (packed[0:3], packed[3:6], packed[6:9], packed[9:12])  1.42 us

profile of v2, /device:TPU:0, one launch (start us, length us, event | category | flops | bytes accessed | tf_op | source)
XLA Modules:
  0.0 39.5 jit_solution(4725104382185259467)
XLA Ops:
  0.6 37.4 %shard_map.75 = f32[12,256]{1,0:T(8,128)} custom-call(f32[3,2048]{1,0:T(4,128)} %pos_ref.1, f32[3,2048]{1,0:T(4,128)} %vel_ref.1, f32[1,2048]{1,0:T(1,128)} %bitcast.2, s32[1,256]{1,0:T(1,128)} %bitcast.3), custom_call_target="tpu_custom_call" | custom-call | tf_op jit(solution)/shard_map/pallas_call | solution.py:220
  38.1 1.4 %fusion = (f32[3,256]{1,0:T(4,128)}, f32[3,256]{1,0:T(4,128)}, f32[3,256]{1,0:T(4,128)}, f32[3,256]{1,0:T(4,128)}) fusion(f32[12,256]{1,0:T(8,128)} %shard_map.75), kind=kLoop, calls=%fused_computation | loop fusion | bytes 24576 | tf_op jit(solution)/shard_map/slice | solution.py:238

commit v3 on v2

v3 whole, which is shorter than its diff:
```python
import functools

import jax
import jax.numpy as jnp
from jax import lax
from jax.experimental import pallas as pl
from jax.experimental.pallas import tpu as pltpu
from jax.sharding import PartitionSpec as P

STEPS = 2
TIME_STEP = 0.03125
ROWS = 32
F32 = jnp.float32
BF16 = jnp.bfloat16


def split3(value):
    high = value.astype(BF16)
    rest = value - high.astype(F32)
    middle = rest.astype(BF16)
    low = (rest - middle.astype(F32)).astype(BF16)
    return [high, middle, low]


def kernel(
    n,
    pos_ref,
    vel_ref,
    mass_ref,
    idx_ref,
    out_ref,
    slots,
    target,
    total,
    send_sem,
    recv_sem,
):
    me = lax.axis_index("blk")
    act = idx_ref.shape[1]
    stars = pos_ref.shape[1]

    half = n // 2
    core = me % 2

    chip = me // 2
    partner = me + 1 - 2 * core
    lead = min(4, (half - 1) // 2 * 2)

    def same_core(order, sign):
        offset = sign * ((order + 1) // 2) * (2 * (order % 2) - 1)
        return 2 * lax.rem(chip + (offset + half) % half, half) + core

    barrier = pltpu.get_barrier_semaphore()

    for peer in [partner] + [same_core(order, 1) for order in range(1, half)]:
        pl.semaphore_signal(
            barrier, inc=1, device_id={"blk": peer}, device_id_type=pl.DeviceIdType.MESH
        )

    local_idx = idx_ref[...] - me * stars
    table = jnp.concatenate(
        [pos_ref[...], vel_ref[...], mass_ref[...], jnp.zeros((1, stars), F32)], axis=0
    )
    pieces = jnp.concatenate(split3(table), axis=0)
    picked = (lax.broadcasted_iota(jnp.int32, (stars, act), 0) == local_idx).astype(F32).astype(BF16)
    found = jnp.dot(pieces, picked, preferred_element_type=F32)
    own = found[0:8] + found[8:16] + found[16:24]
    mass_rows = own[6:8]

    pl.semaphore_wait(barrier, half)

    def copy_to(step, source, place, peer):
        return pltpu.make_async_remote_copy(
            src_ref=slots.at[step, source],
            dst_ref=slots.at[step, place],
            send_sem=send_sem.at[step, place],
            recv_sem=recv_sem.at[step, place],
            device_id={"blk": peer},
            device_id_type=pl.DeviceIdType.MESH,
        )

    def wait_at(step, place):
        copy_to(step, place, place, partner).wait_recv()

        @pl.when((place > 1) & (place <= half))
        def _():
            copy_to(step, place, place + half - 1, partner).start()

    row_id = lax.broadcasted_iota(jnp.int32, (8, act), 0)

    def add_pair(blocks, centre, fine):
        right = []
        for block in blocks:
            factor = jnp.where(row_id == 6, 1.0, block - centre)
            right.append(jnp.concatenate(split3(factor * block[6:7]), axis=0))
        right = jnp.concatenate(right + right if fine else right, axis=1)
        for top in range(0, act, ROWS):
            rows = slice(top, top + ROWS)
            highs, lows = [], []
            for block in blocks:
                for side in range(0, act, 128):
                    src = [block[c : c + 1, side : side + 128] for c in range(6)]
                    d = [src[c] - target[c, rows, :] for c in range(3)]
                    e = [src[c + 3] - target[c + 3, rows, :] for c in range(3)]
                    squared = d[0] * d[0] + d[1] * d[1] + d[2] * d[2] + 0.0025
                    radial = d[0] * e[0] + d[1] * e[1] + d[2] * e[2]
                    inverse = lax.rsqrt(squared)
                    inverse2 = inverse * inverse
                    w = inverse2 * inverse
                    both = jnp.concatenate([w, w * inverse2 * radial], axis=0)
                    high = both.astype(BF16)
                    highs.append(high)
                    if fine:
                        lows.append((both - high.astype(F32)).astype(BF16))
            total[2 * top : 2 * top + 2 * ROWS] += lax.dot_general(
                jnp.concatenate(highs + lows, axis=1),
                right,
                (((1,), (1,)), ((), ())),
                preferred_element_type=F32,
            )

    def field(step, own):
        fine = step == STEPS
        slots[step, 0] = own
        for order in range(half - 1, 0, -1):
            copy_to(step, 0, 1 + order, same_core(order, -1)).start()
        copy_to(step, 0, 1, partner).start()

        columns = own.T
        for c in range(6):
            target[c] = jnp.broadcast_to(columns[:, c : c + 1], (act, 128))
        centre = jnp.where(row_id[:, 0:1] < 6, jnp.mean(own, axis=1, keepdims=True), 0.0)
        total[...] = jnp.zeros_like(total)

        @pl.loop(0, n // 2)
        def _(pair):
            middle = (pair > lead // 2) & (pair < (n - lead) // 2)
            first = jnp.where(middle, half + pair - lead // 2, 2 * pair)
            second = jnp.where(middle, 1 + lead + pair - lead // 2, 2 * pair + 1)

            @pl.when(pair > 0)
            def _():
                wait_at(step, first)

            wait_at(step, second)
            add_pair([slots[step, first], slots[step, second]], centre, fine)

        sums = total[...].T
        sums = sums[0:8] + sums[8:16] + sums[16:24]
        tops = range(0, 2 * act, 2 * ROWS)
        plain = jnp.concatenate([sums[:, t : t + ROWS] for t in tops], axis=1)
        scaled = jnp.concatenate([sums[:, t + ROWS : t + 2 * ROWS] for t in tops], axis=1)
        about = own - centre
        accel = plain[0:3] - about[0:3] * plain[6:7]
        jerk = (
            plain[3:6]
            - about[3:6] * plain[6:7]
            - 3.0 * (scaled[0:3] - about[0:3] * scaled[6:7])
        )
        return accel, jerk

    pos, vel = own[0:3], own[3:6]
    accel, jerk = field(0, own)
    h = TIME_STEP
    for step in range(STEPS):
        pred_pos = pos + h * vel + h**2 / 2.0 * accel + h**3 / 6.0 * jerk
        pred_vel = vel + h * accel + h**2 / 2.0 * jerk
        accel_new, jerk_new = field(
            step + 1, jnp.concatenate([pred_pos, pred_vel, mass_rows], axis=0)
        )
        vel_new = vel + h / 2.0 * (accel + accel_new) + h**2 / 12.0 * (jerk - jerk_new)
        pos = pos + h / 2.0 * (vel + vel_new) + h**2 / 12.0 * (accel - accel_new)
        vel, accel, jerk = vel_new, accel_new, jerk_new
    out_ref[...] = jnp.concatenate([pos, vel, accel, jerk], axis=0)

    for step in range(STEPS + 1):

        @pl.loop(1, n)
        def _(place):
            copy_to(step, 0, place, partner).wait_send()


def solution(mesh):
    n = mesh.shape["blk"]

    def shards(positions, velocities, masses, active):
        act = active.shape[0]
        vmem = pl.BlockSpec(memory_space=pltpu.VMEM)
        packed = pl.pallas_call(
            functools.partial(kernel, n),
            out_shape=jax.ShapeDtypeStruct((12, act), F32),
            in_specs=[vmem] * 4,
            out_specs=vmem,
            scratch_shapes=[
                pltpu.VMEM((STEPS + 1, n, 8, act), F32),
                pltpu.VMEM((6, act, 128), F32),
                pltpu.VMEM((2 * act, 24), F32),
                pltpu.SemaphoreType.DMA((STEPS + 1, n)),
                pltpu.SemaphoreType.DMA((STEPS + 1, n)),
            ],
            compiler_params=pltpu.CompilerParams(collective_id=0, has_side_effects=True),
        )(positions, velocities, masses.reshape(1, -1), active.reshape(1, -1))
        return packed[0:3], packed[3:6], packed[6:9], packed[9:12]

    spec = P(None, ("clusters", "blk"))
    flat = P(("clusters", "blk"))
    return jax.shard_map(
        shards,
        mesh=mesh,
        in_specs=(spec, spec, flat, flat),
        out_specs=(spec, spec, spec, spec),
        check_vma=False,
    )
```

time: 39.7 us -> 35.6 us (0.90)
  Pallas kernels: 37.4 us -> 33.3 us
    pallas_call x1, Pallas kernels: 37.4 us -> 33.3 us  [shards(): pl.pallas_call(functools.partial(kernel, n), out_shape=jax.ShapeDtypeStru...]
where the time goes in v3:
time: 35.6 us; the launch traced here: 35.4 us
  Pallas kernels  33.3 us (94%)
  local copies, waits for them, and re-layouts  1.42 us (4%)
  between operations  0.64 us (2%)
    pallas_call x1, Pallas kernels, shards(): pl.pallas_call(functools.partial(kernel, n), out_shape=jax.ShapeDtypeStru...  33.3 us
    slice x1, local copies, waits for them, and re-layouts, shards(): return (packed[0:3], packed[3:6], packed[6:9], packed[9:12])  1.42 us

profile of v3, /device:TPU:0, one launch (start us, length us, event | category | flops | bytes accessed | tf_op | source)
XLA Modules:
  0.0 35.4 jit_solution(3779937095810559286)
XLA Ops:
  0.6 33.3 %shard_map.75 = f32[12,256]{1,0:T(8,128)} custom-call(f32[3,2048]{1,0:T(4,128)} %pos_ref.1, f32[3,2048]{1,0:T(4,128)} %vel_ref.1, f32[1,2048]{1,0:T(1,128)} %bitcast.2, s32[1,256]{1,0:T(1,128)} %bitcast.3), custom_call_target="tpu_custom_call" | custom-call | tf_op jit(solution)/shard_map/pallas_call | solution.py:189
  34.0 1.4 %fusion = (f32[3,256]{1,0:T(4,128)}, f32[3,256]{1,0:T(4,128)}, f32[3,256]{1,0:T(4,128)}, f32[3,256]{1,0:T(4,128)}) fusion(f32[12,256]{1,0:T(8,128)} %shard_map.75), kind=kLoop, calls=%fused_computation | loop fusion | bytes 24576 | tf_op jit(solution)/shard_map/slice | solution.py:203
